TPU v7x, 32 devices: a whole 2x2x4 slice. The times are simulated.
32 devices in a mesh: grp: 4 (over y, x), dev: 8 (over z, core).
Axes of the slice: x: 2, y: 2, z: 4, core: 2. Of those that a mesh axis runs over, the one named last changes fastest.
Arguments:
- table: float32 [262144, 128], P(('grp', 'dev')), may hold values from -6 to 6
- cold_grads: float32 [131072, 128], P(('grp', 'dev')), may hold values from -6 to 6
- cold_owner: int32 [131072, 1], P(('grp', 'dev')), may hold values from 0 to 31; in each aligned block of 4096 rows (0 to 4095, 4096 to 8191, ...) at most 256 rows name the same one
- cold_row: int32 [131072], P(('grp', 'dev')), may hold values from 0 to 8191
- hot_grads: float32 [32768, 128], P(('grp', 'dev')), may hold values from -6 to 6
- hot_slot: int32 [32768], P(('grp', 'dev')), may hold values from 0 to 255
- hot_ids: int32 [256], replicated, may hold values from 0 to 262143, as said below
Outputs:
- new_table: float32 [262144, 128], P(('grp', 'dev'))
Inputs may be any that keep to these rules, and one draw needn't show every extreme that they name: `cold_owner`: among the 4096 rare-row lookups of one device no owner is named more than 256 times, a bound that some block reaches. `hot_ids`: all entries differ.
All inputs are finite; a program needn't handle non-finite values.
Results may differ from a plain program's by a relative error of at most 0.00005.
Values sent between devices are 32-bit elements; how exact they have to be, the bound alone decides.
A program may use at most 64 MiB of HBM per device.

v0:
```python
import jax
import jax.numpy as jnp
from jax import lax
from jax.sharding import PartitionSpec as P

LEARN = 0.05


def hot_update(table, hot_grads, hot_slot, hot_ids):
    count = hot_ids.shape[0]
    pick = (jnp.arange(count, dtype=jnp.int32)[:, None] == hot_slot[None, :]).astype(jnp.float32)
    partial_sum = jnp.dot(
        pick, hot_grads, precision=lax.Precision.HIGHEST, preferred_element_type=jnp.float32
    )
    share = lax.psum_scatter(partial_sum, "dev", scatter_dimension=0, tiled=True)
    share = lax.psum(share, "grp")
    total = lax.all_gather(share, "dev", axis=0, tiled=True)
    rows_dev = table.shape[0]
    local = hot_ids - lax.axis_index(("grp", "dev")) * rows_dev
    inside = (local >= 0) & (local < rows_dev)
    target = jnp.where(inside, local, rows_dev)
    return table.at[target].add(-LEARN * total, mode="drop")


def pack_cold(cold_grads, cold_owner, cold_row, devices, slots):
    owner = cold_owner[:, 0]
    onehot = (owner[:, None] == jnp.arange(devices, dtype=jnp.int32)[None, :]).astype(jnp.int32)
    running = jnp.cumsum(onehot, axis=0) - 1
    rank = jnp.sum(running * onehot, axis=1)
    target = owner * slots + rank
    width = cold_grads.shape[1]
    send_grads = jnp.zeros((devices * slots, width), jnp.float32).at[target].set(cold_grads)
    send_rows = jnp.zeros((devices * slots,), jnp.int32).at[target].set(cold_row)
    return (send_grads, send_rows)


def on_device(table, cold_grads, cold_owner, cold_row, hot_grads, hot_slot, hot_ids):
    n_grp = lax.axis_size("grp")
    n_dev = lax.axis_size("dev")
    devices = n_grp * n_dev
    width = table.shape[1]
    slots = max(4, 2 * cold_grads.shape[0] // devices)
    send_grads, send_rows = pack_cold(cold_grads, cold_owner, cold_row, devices, slots)
    grads_four = send_grads.reshape(n_grp, n_dev, slots, width)
    rows_three = send_rows.reshape(n_grp, n_dev, slots)
    got_grads, got_rows = (
        lax.all_to_all(
            lax.all_to_all(grads_four, "grp", split_axis=0, concat_axis=0, tiled=True),
            "dev",
            split_axis=1,
            concat_axis=1,
            tiled=True,
        ),
        lax.all_to_all(
            lax.all_to_all(rows_three, "grp", split_axis=0, concat_axis=0, tiled=True),
            "dev",
            split_axis=1,
            concat_axis=1,
            tiled=True,
        ),
    )
    current = hot_update(table, hot_grads, hot_slot, hot_ids)
    current = current.at[got_rows.reshape(-1)].add(-LEARN * got_grads.reshape(-1, width))
    return current


def solution(mesh):
    in_specs = (
        P(("grp", "dev"), None),
        P(("grp", "dev"), None),
        P(("grp", "dev"), None),
        P(("grp", "dev")),
        P(("grp", "dev"), None),
        P(("grp", "dev")),
        P(),
    )
    out_specs = P(("grp", "dev"), None)
    return jax.shard_map(
        on_device, mesh=mesh, in_specs=in_specs, out_specs=out_specs, check_vma=False
    )
```

profile of v0, /device:TPU:13, one launch (start us, length us, event | category | flops | bytes accessed | tf_op | source)
XLA Modules:
  0.0 297.8 jit_solution(3252168921994145079)
XLA Ops:
  6.5 0.0 copy-start
  6.5 0.0 copy-start.1
  6.5 4.5 %copy.23 = f32[8192,128]{1,0:T(8,128)} copy(f32[8192,128]{1,0:T(8,128)} %param.7) | data formatting | bytes 8388608
  11.1 0.0 copy-done.1
  11.1 0.1 fusion.6
  11.1 9.2 %reduce-window.6 = s32[32,32,128]{2,1,0:T(8,128)S(1)} reduce-window(s32[32,32,128]{2,1,0:T(8,128)S(1)} %fusion.6, s32[]{:T(128)} %constant.13.clone.1), window={size=1x1x128 pad=0_0x0_0x127_0}, to_apply=%region_3.4 | reduce-window | flops 16646144 | bytes 1048580 | tf_op jit(solution)/shard_map/reduce-window
  20.4 0.8 slice_reduce_fusion
  21.2 0.2 reduce-window.9
  21.4 0.2 add_add_fusion
  21.6 0.3 fusion.4
  21.9 15.7 %scatter_custom_fusion.1 = s32[8192]{0:T(1024)S(1)} fusion(s32[4096]{0:T(1024)S(1)} %bitcast.30, s32[4096]{0:T(1024)} %param.10, s32[]{:T(128)} %constant.13.clone.1), kind=kCustom, calls=%fused_computation.23 | custom fusion | bytes 33280 | tf_op jit(solution)/shard_map/scatter | solution.py:33
  37.7 0.6 reshape.61
  38.3 3.7 %all-to-all-start = ((s32[4,8,256]{2,1,0:T(8,128)}), s32[4,8,256]{2,1,0:T(8,128)S(1)}, u32[]{:S(2)}, u32[]{:S(2)}) async-start(s32[4,8,256]{2,1,0:T(8,128)} %reshape.61), calls=%async_computation.1 | async-start | bytes 65536 | tf_op jit(solution)/shard_map/all_to_all | solution.py:55
  41.9 13.1 %scatter_custom_fusion.2 = f32[8192,128]{1,0:T(8,128)} fusion(s32[4096]{0:T(1024)S(1)} %bitcast.31, f32[4096,128]{1,0:T(8,128)} %param.8, f32[]{:T(128)} %constant.17.clone.1), kind=kCustom, calls=%fused_computation.5 | custom fusion | bytes 4194816 | tf_op jit(solution)/shard_map/scatter | solution.py:32
  55.0 0.0 all-to-all-done
  55.0 4.9 %all-to-all-start.2 = ((f32[4,8,256,128]{3,2,1,0:T(8,128)}), f32[4,8,256,128]{3,2,1,0:T(8,128)}, u32[]{:S(2)}, u32[]{:S(2)}) async-start(f32[4,8,256,128]{3,2,1,0:T(8,128)} %bitcast.23), calls=%async_computation.3 | async-start | bytes 8388608 | tf_op jit(solution)/shard_map/all_to_all | solution.py:48
  59.9 0.6 copy.13
  60.5 45.7 %all-to-all-done.2 = f32[4,8,256,128]{3,2,1,0:T(8,128)} async-done(((f32[4,8,256,128]{3,2,1,0:T(8,128)}), f32[4,8,256,128]{3,2,1,0:T(8,128)}, u32[]{:S(2)}, u32[]{:S(2)}) %all-to-all-start.2) | async-done | bytes 4194336 | tf_op jit(solution)/shard_map/all_to_all | solution.py:48
  106.2 6.7 %all-to-all-start.1 = ((s32[4,8,256]{2,0,1:T(4,128)}), s32[4,8,256]{2,0,1:T(4,128)S(1)}, u32[]{:S(2)}, u32[]{:S(2)}) async-start(s32[4,8,256]{2,0,1:T(4,128)} %copy.13), calls=%async_computation.2 | async-start | bytes 65536 | tf_op jit(solution)/shard_map/all_to_all | solution.py:54
  112.9 4.6 %copy.15 = f32[4,8,256,128]{3,2,0,1:T(8,128)} copy(f32[4,8,256,128]{3,2,1,0:T(8,128)} %all-to-all-done.2) | data formatting | bytes 8388608 | tf_op jit(solution)/shard_map/all_to_all | solution.py:48
  117.4 0.0 copy-start.2
  117.4 0.0 copy-start.3
  117.4 0.0 all-to-all-done.1
  117.4 5.6 %all-to-all-start.3 = ((f32[4,8,256,128]{3,2,0,1:T(8,128)}), f32[4,8,256,128]{3,2,0,1:T(8,128)}, u32[]{:S(2)}, u32[]{:S(2)}) async-start(f32[4,8,256,128]{3,2,0,1:T(8,128)} %copy.15), calls=%async_computation.4 | async-start | bytes 8388608 | tf_op jit(solution)/shard_map/all_to_all | solution.py:47
  123.0 0.0 reduce-scatter.2.cloned.1.call-start
  123.0 0.0 copy-done
  123.1 0.0 copy-done.2
  123.1 1.3 fusion.2
  124.4 0.0 reduce-scatter.2.cloned.1.call-update
  124.4 0.0 copy-done.3
  124.6 28.5 %reduce-scatter.2.cloned.1.call-done = f32[32,128]{1,0:T(8,128)} async-done(((f32[256,128]{1,0:T(8,128)}), f32[32,128]{1,0:T(8,128)}) %reduce-scatter.2.cloned.1.call-update) | async-done | bytes 16400 | tf_op jit(solution)/shard_map/reduce_scatter | solution.py:15
  153.1 11.9 %psum.7 = f32[32,128]{1,0:T(8,128)S(1)} all-reduce(f32[32,128]{1,0:T(8,128)} %reduce-scatter.2.cloned.1.call-done), channel_id=1, replica_groups=mesh['grp'=4,'dev'=8] {'grp'}, use_global_device_ids=true, to_apply=%region_1.2 | all-reduce | flops 4096 | bytes 32768 | tf_op jit(solution)/shard_map/psum | solution.py:16
  165.0 58.6 %all_gather.3 = f32[256,128]{1,0:T(8,128)S(1)} all-gather(f32[32,128]{1,0:T(8,128)S(1)} %psum.7), channel_id=1, replica_groups=mesh['grp'=4,'dev'=8] {'dev'}, dimensions={0}, use_global_device_ids=true | all-gather | bytes 147456 | tf_op jit(solution)/shard_map/all_gather | solution.py:17
  223.6 6.0 %scatter_custom_fusion = f32[8192,128]{1,0:T(8,128)} fusion(f32[8192,128]{1,0:T(8,128)} %copy.23, s32[256]{0:T(256)S(1)} %compare_select_fusion.2, f32[256,128]{1,0:T(8,128)S(1)} %all_gather.3, f32[]{:T(128)} %constant.14.clone.1), kind=kCustom, calls=%fused_computation.19 | custom fusion | flops 65536 | bytes 4325888 | tf_op jit(solution)/shard_map/scatter-add | solution.py:22
  229.6 0.0 all-to-all-done.3
  229.6 4.7 %copy_multiply_fusion = f32[4,8,256,128]{3,2,1,0:T(8,128)} fusion(f32[4,8,256,128]{3,2,0,1:T(8,128)} %all-to-all-done.3), kind=kLoop, calls=%fused_computation.4 | loop fusion | flops 1048576 | bytes 8388608 | tf_op jit(solution)/shard_map/mul | solution.py:63
  234.3 56.7 %scatter_fusion = f32[8192,128]{1,0:T(8,128)} fusion(f32[8192,128]{1,0:T(8,128)} %scatter_custom_fusion, s32[8192]{0:T(1024)S(1)} %bitcast.27, f32[8192,128]{1,0:T(8,128)} %bitcast.22), kind=kCustom, calls=%fused_computation.3 | custom fusion | flops 1048576 | bytes 12615680 | tf_op jit(solution)/shard_map/scatter-add | solution.py:63
  (5 shorter events, 0.1 us)
Async XLA Ops:
  6.5 116.5 %copy-start = (f32[1024,128]{1,0:T(8,128)S(1)}, f32[1024,128]{1,0:T(8,128)}, u32[]{:S(2)}) copy-start(f32[1024,128]{1,0:T(8,128)} %param.11) | copy-start | bytes 1572868
  6.5 4.5 %copy-start.1 = (s32[4096,1]{0,1:T(1,128)S(1)}, s32[4096,1]{0,1:T(1,128)}, u32[]{:S(2)}) copy-start(s32[4096,1]{0,1:T(1,128)} %param.9) | copy-start | bytes 49156
  38.3 16.7 %all-to-all-start = ((s32[4,8,256]{2,1,0:T(8,128)}), s32[4,8,256]{2,1,0:T(8,128)S(1)}, u32[]{:S(2)}, u32[]{:S(2)}) async-start(s32[4,8,256]{2,1,0:T(8,128)} %reshape.61), calls=%async_computation.1 | async-start | bytes 65536 | tf_op jit(solution)/shard_map/all_to_all | solution.py:55
  55.0 51.2 %all-to-all-start.2 = ((f32[4,8,256,128]{3,2,1,0:T(8,128)}), f32[4,8,256,128]{3,2,1,0:T(8,128)}, u32[]{:S(2)}, u32[]{:S(2)}) async-start(f32[4,8,256,128]{3,2,1,0:T(8,128)} %bitcast.23), calls=%async_computation.3 | async-start | bytes 8388608 | tf_op jit(solution)/shard_map/all_to_all | solution.py:48
  106.2 11.3 %all-to-all-start.1 = ((s32[4,8,256]{2,0,1:T(4,128)}), s32[4,8,256]{2,0,1:T(4,128)S(1)}, u32[]{:S(2)}, u32[]{:S(2)}) async-start(s32[4,8,256]{2,0,1:T(4,128)} %copy.13), calls=%async_computation.2 | async-start | bytes 65536 | tf_op jit(solution)/shard_map/all_to_all | solution.py:54
  117.4 5.6 %copy-start.2 = (s32[1024]{0:T(1024)S(1)}, s32[1024]{0:T(1024)}, u32[]{:S(2)}) copy-start(s32[1024]{0:T(1024)} %param.12) | copy-start | bytes 12292
  117.4 7.0 %copy-start.3 = (s32[256]{0:T(256)S(1)}, s32[256]{0:T(256)}, u32[]{:S(2)}) copy-start(s32[256]{0:T(256)} %param.13) | copy-start | bytes 3076
  117.4 112.1 %all-to-all-start.3 = ((f32[4,8,256,128]{3,2,0,1:T(8,128)}), f32[4,8,256,128]{3,2,0,1:T(8,128)}, u32[]{:S(2)}, u32[]{:S(2)}) async-start(f32[4,8,256,128]{3,2,0,1:T(8,128)} %copy.15), calls=%async_computation.4 | async-start | bytes 8388608 | tf_op jit(solution)/shard_map/all_to_all | solution.py:47
  123.0 30.0 %reduce-scatter.2.cloned.1.call-start = ((), (), s32[]{:S(2)}) async-start(), calls=%async_computation.5 | async-start | bytes 147456 | tf_op jit(solution)/shard_map/reduce_scatter | solution.py:15
Sparse Core Ops, SparseCore 0:
  126.1 26.9 reduce-scatter.1
where the time goes:
time: 300 us; the launch traced here: 298 us
  other arithmetic  77.4 us (26%)
  waiting for transfers between devices  74.2 us (25%)
  blocking collectives  70.5 us (24%)
  local copies, waits for them, and re-layouts  39.9 us (13%)
  starting transfers between devices  20.8 us (7%)
  between operations  13.5 us (4%)
    all_gather x1, blocking collectives, hot_update(): total = lax.all_gather(share, 'dev', axis=0, tiled=True)  58.6 us
    scatter-add x1, other arithmetic, on_device(): current.at[got_rows.reshape(-1)].add(-LEARN * got_grads.reshape(-1, width))  56.7 us
    all_to_all x1, waiting for transfers between devices, on_device(): lax.all_to_all(grads_four, 'grp', split_axis=0, concat_axis=0, tiled=True)  45.7 us
    reduce_scatter x1, waiting for transfers between devices, hot_update(): lax.psum_scatter(partial_sum, 'dev', scatter_dimension=0, tiled=True)  28.5 us
    scatter x1, local copies, waits for them, and re-layouts, pack_cold(): jnp.zeros((devices * slots,), jnp.int32).at[target].set(cold_row)  15.7 us
    scatter x1, local copies, waits for them, and re-layouts, pack_cold(): jnp.zeros((devices * slots, width), jnp.float32).at[target].set(cold_grads)  13.1 us
    psum x1, blocking collectives, hot_update(): share = lax.psum(share, 'grp')  11.9 us
    another operation x2, other arithmetic  9.41 us
  transfers between devices with their start and end apart: 5, of which 2 were waited for; matrix products, arithmetic and copies ran while one was open for 9% of the time, Pallas kernels for 0%

commit v1 on v0

v1 whole, which is shorter than its diff:
```python
import functools

import jax
import jax.numpy as jnp
from jax import lax
from jax.experimental import pallas as pl
from jax.experimental.pallas import tpu as pltpu
from jax.sharding import PartitionSpec as P

LEARN = 0.05
MESH = pl.DeviceIdType.MESH
LANES = 128
CHUNK = 256
WAYS = 4
TILE = 1024


def plan_kernel(slots, owner_ref, hot_grads_ref, hot_slot_ref, place_ref, count_ref, partial_ref):
    lookups = owner_ref.shape[0]
    wide = count_ref.shape[1]
    above = lax.broadcasted_iota(jnp.int32, (CHUNK, CHUNK), 0)
    below = lax.broadcasted_iota(jnp.int32, (CHUNK, CHUNK), 1)
    tri = (above >= below).astype(jnp.bfloat16)
    owners = lax.broadcasted_iota(jnp.int32, (CHUNK, wide), 1)
    start = owners.astype(jnp.float32) * slots - 1.0
    ones = jnp.ones((8, wide), jnp.float32)
    base = jnp.zeros((1, wide), jnp.float32)
    for b in range(lookups // CHUNK):
        hit = owner_ref[b * CHUNK:(b + 1) * CHUNK, :] == owners
        run = jnp.dot(tri, hit.astype(jnp.bfloat16), preferred_element_type=jnp.float32) + base
        base = run[CHUNK - 1:CHUNK, :]
        chosen = jnp.where(hit, run + start, 0.0)
        flat = lax.dot_general(
            ones, chosen, (((1,), (1,)), ((), ())),
            precision=lax.Precision.HIGHEST, preferred_element_type=jnp.float32,
        )
        whole = (flat + 0.5).astype(jnp.int32)
        for j in range(CHUNK // LANES):
            r = b * (CHUNK // LANES) + j
            place_ref[r:r + 1, :] = whole[0:1, j * LANES:(j + 1) * LANES]
    count_ref[...] = jnp.broadcast_to((base + 0.5).astype(jnp.int32), count_ref.shape)
    hot = partial_ref.shape[0]
    looks = hot_grads_ref.shape[0]
    pick = lax.broadcasted_iota(jnp.int32, (hot, looks), 0) == hot_slot_ref[...]
    partial_ref[...] = jnp.dot(
        pick.astype(jnp.float32), hot_grads_ref[...],
        precision=lax.Precision.HIGHEST, preferred_element_type=jnp.float32,
    )


def pack_kernel(place_ref, row_ref, grads_ref, send_ref, rows_ref):
    step = 16

    def body(t, carry):
        first = pl.multiple_of(t * step, step)
        for j in range(step):
            to = place_ref[first + j]
            rows_ref[to] = row_ref[first + j]
            send_ref[pl.ds(to, 1), :] = grads_ref[pl.ds(first + j, 1), :]
        return carry

    lax.fori_loop(0, grads_ref.shape[0] // step, body, 0)


def exchange_kernel(
    n_grp, n_dev, send_ref, meta_ref, part_ref, got_ref, gmeta_ref, total_ref,
    rbuf, s_big, r_big, s_meta, r_meta, s_rs, r_rs, s_ag, r_ag, s_own,
):
    devices = n_grp * n_dev
    me = lax.axis_index("grp") * n_dev + lax.axis_index("dev")
    barrier = pltpu.get_barrier_semaphore()

    def peer(k):
        p = lax.rem(me + k, devices)
        return p, (p // n_dev, lax.rem(p, n_dev))

    def each(fn):
        def body(k, carry):
            fn(*peer(k))
            return carry
        lax.fori_loop(1, devices, body, 0)

    def remote(src, dst, ssem, rsem, where):
        return pltpu.make_async_remote_copy(
            src_ref=src, dst_ref=dst, send_sem=ssem, recv_sem=rsem,
            device_id=where, device_id_type=MESH,
        )

    each(lambda p, w: pl.semaphore_signal(barrier, inc=1, device_id=w, device_id_type=MESH))
    pl.semaphore_wait(barrier, devices - 1)

    each(lambda p, w: remote(part_ref.at[p], rbuf.at[me], s_rs, r_rs, w).start())
    each(lambda p, w: remote(meta_ref.at[p], gmeta_ref.at[me], s_meta, r_meta, w).start())
    each(lambda p, w: remote(send_ref.at[p], got_ref.at[me], s_big, r_big, w).start())
    own_big = pltpu.make_async_copy(send_ref.at[me], got_ref.at[me], s_own.at[0])
    own_meta = pltpu.make_async_copy(meta_ref.at[me], gmeta_ref.at[me], s_own.at[1])
    own_big.start()
    own_meta.start()
    rbuf[me] = part_ref[me]

    here = (lax.axis_index("grp"), lax.axis_index("dev"))
    most = pl.ds(0, devices - 1)

    def all_of(src, dst, ssem, rsem):
        return remote(src.at[most], dst.at[most], ssem, rsem, here)

    rs = all_of(part_ref, rbuf, s_rs, r_rs)
    rs.wait_recv()
    total_ref[me] = jnp.sum(rbuf[...], axis=0)
    rs.wait_send()
    each(lambda p, w: remote(total_ref.at[me], total_ref.at[me], s_ag, r_ag, w).start())
    for t in (
        all_of(meta_ref, gmeta_ref, s_meta, r_meta),
        all_of(send_ref, got_ref, s_big, r_big),
        all_of(total_ref, total_ref, s_ag, r_ag),
    ):
        t.wait_send()
        t.wait_recv()
    own_big.wait()
    own_meta.wait()


def apply_kernel(
    slots, rows_ref, count_ref, local_ref, table_ref, got_ref, hot_ref, out_ref,
    grads, base, acc, g_sem, t_sem, o_sem,
):
    devices = got_ref.shape[0]
    rows_dev = table_ref.shape[0]
    for s in range(devices):
        pltpu.make_async_copy(got_ref.at[s], grads.at[s], g_sem.at[s]).start()
    load = pltpu.make_async_copy(table_ref, base, t_sem)
    load.start()

    def clear(t, carry):
        r = pl.ds(pl.multiple_of(t * 64, 64), 64)
        for a in acc:
            a[r, :] = jnp.zeros((64, a.shape[1]), jnp.float32)
        return carry

    lax.fori_loop(0, rows_dev // 64, clear, 0)

    def add(pairs):
        olds = [acc[j % WAYS][pl.ds(i, 1), :] for j, (i, _) in enumerate(pairs)]
        news = [o + g() for o, (_, g) in zip(olds, pairs)]
        for j, ((i, _), v) in enumerate(zip(pairs, news)):
            acc[j % WAYS][pl.ds(i, 1), :] = v

    def source(s, carry):
        pltpu.make_async_copy(got_ref.at[s], grads.at[s], g_sem.at[s]).wait()
        n = count_ref[s]
        first = s * slots

        def entry(i):
            return rows_ref[first + i], lambda: grads[s, pl.ds(i, 1), :]

        def four(t, c):
            for u in range(2):
                add([entry(t * 2 * WAYS + u * WAYS + j) for j in range(WAYS)])
            return c

        def one(i, c):
            add([entry(i)])
            return c

        full = n // (2 * WAYS)
        lax.fori_loop(0, full, four, 0)
        lax.fori_loop(full * 2 * WAYS, n, one, 0)
        return carry

    lax.fori_loop(0, devices, source, 0)

    def hot_one(i, c):
        r = local_ref[i]

        @pl.when((r >= 0) & (r < rows_dev))
        def _():
            add([(r, lambda: hot_ref[pl.ds(i, 1), :])])

        return c

    lax.fori_loop(0, local_ref.shape[0], hot_one, 0)
    load.wait()
    parts = 4
    size = rows_dev // parts
    outs = []
    for q in range(parts):
        def finish(t, c):
            r = pl.ds(pl.multiple_of(q * size + t * 64, 64), 64)
            v = acc[0][r, :]
            for a in acc[1:]:
                v = v + a[r, :]
            base[r, :] = base[r, :] - LEARN * v
            return c

        lax.fori_loop(0, size // 64, finish, 0)
        w = pl.ds(q * size, size)
        outs.append(pltpu.make_async_copy(base.at[w], out_ref.at[w], o_sem.at[q]))
        outs[-1].start()
    for o in outs:
        o.wait()


def on_device(n_grp, n_dev, table, cold_grads, cold_owner, cold_row, hot_grads, hot_slot, hot_ids):
    devices = n_grp * n_dev
    width = table.shape[1]
    lookups = cold_grads.shape[0]
    rows_dev = table.shape[0]
    hot = hot_ids.shape[0]
    slots = max(4, 2 * lookups // devices)
    wide = -(-devices // LANES) * LANES
    vmem, smem, hbm = (pl.BlockSpec(memory_space=m) for m in (pltpu.VMEM, pltpu.SMEM, pl.ANY))
    f32, i32 = jnp.float32, jnp.int32
    place, count, partial = pl.pallas_call(
        functools.partial(plan_kernel, slots),
        out_shape=(
            jax.ShapeDtypeStruct((lookups // LANES, LANES), i32),
            jax.ShapeDtypeStruct((8, wide), i32),
            jax.ShapeDtypeStruct((hot, width), f32),
        ),
        in_specs=[vmem] * 3,
        out_specs=(vmem,) * 3,
        name="plan",
    )(cold_owner, hot_grads, hot_slot.reshape(1, -1))
    send, rows = pl.pallas_call(
        pack_kernel,
        out_shape=(
            jax.ShapeDtypeStruct((devices * slots, width), f32),
            jax.ShapeDtypeStruct((devices * slots,), i32),
        ),
        in_specs=[smem, smem, vmem],
        out_specs=(vmem, smem),
        name="pack",
    )(place.reshape(-1), cold_row, cold_grads)
    span = -(-(slots + 1) // TILE) * TILE
    meta = jnp.concatenate(
        [rows.reshape(devices, slots), count[0, :devices, None],
         jnp.zeros((devices, span - slots - 1), i32)], axis=1,
    ).reshape(devices, span // LANES, LANES)
    share = -(-hot // devices)
    partial = jnp.pad(partial, ((0, share * devices - hot), (0, 0))).reshape(devices, share, width)
    dma = pltpu.SemaphoreType.DMA
    got, gmeta, total = pl.pallas_call(
        functools.partial(exchange_kernel, n_grp, n_dev),
        out_shape=(
            jax.ShapeDtypeStruct((devices, slots, width), f32),
            jax.ShapeDtypeStruct(meta.shape, i32),
            jax.ShapeDtypeStruct(partial.shape, f32),
        ),
        in_specs=[hbm, hbm, vmem],
        out_specs=(hbm, hbm, vmem),
        scratch_shapes=[pltpu.VMEM(partial.shape, f32)] + [dma] * 8 + [dma((2,))],
        compiler_params=pltpu.CompilerParams(collective_id=0, has_side_effects=True),
        name="exchange",
    )(send.reshape(devices, slots, width), meta, partial)
    gflat = gmeta.reshape(devices, span)
    me = lax.axis_index("grp") * n_dev + lax.axis_index("dev")
    return pl.pallas_call(
        functools.partial(apply_kernel, slots),
        out_shape=jax.ShapeDtypeStruct(table.shape, f32),
        in_specs=[smem, smem, smem, hbm, hbm, vmem],
        out_specs=hbm,
        scratch_shapes=[
            pltpu.VMEM(got.shape, f32),
            pltpu.VMEM(table.shape, f32),
            [pltpu.VMEM(table.shape, f32) for _ in range(WAYS)],
            dma((devices,)), dma, dma((4,)),
        ],
        compiler_params=pltpu.CompilerParams(vmem_limit_bytes=48 * 1024 * 1024),
        name="apply",
    )(gflat[:, :slots].reshape(-1), gflat[:, slots], hot_ids - me * rows_dev,
      table, got, total.reshape(-1, width))


def solution(mesh):
    in_specs = (
        P(("grp", "dev"), None),
        P(("grp", "dev"), None),
        P(("grp", "dev"), None),
        P(("grp", "dev")),
        P(("grp", "dev"), None),
        P(("grp", "dev")),
        P(),
    )
    out_specs = P(("grp", "dev"), None)
    return jax.shard_map(
        functools.partial(on_device, mesh.shape["grp"], mesh.shape["dev"]),
        mesh=mesh, in_specs=in_specs, out_specs=out_specs, check_vma=False,
    )
```

time: 300 us -> 162 us (0.54)
  Pallas kernels: 0 us -> 150 us
  other arithmetic: 77.4 us -> 0.02 us
  waiting for transfers between devices: 74.2 us -> 0 us
  blocking collectives: 70.5 us -> 0 us
  local copies, waits for them, and re-layouts: 39.9 us -> 9.1 us
  starting transfers between devices: 20.8 us -> 0 us
  between operations: 13.5 us -> 0.06 us
    pallas_call x0 -> x4, Pallas kernels: none -> 150 us  [the longest x1 108 us: on_device(): pl.pallas_call(functools.partial(exchange_kernel, n_grp, n_dev), out_shap...]
    scatter-add x2 -> x0, other arithmetic: 62.7 us -> none  [the longest x1 56.7 us: on_device(): current.at[got_rows.reshape(-1)].add(-LEARN * got_grads.reshape(-1, width))]
    all_gather x1 -> x0, blocking collectives: 58.6 us -> none  [hot_update(): total = lax.all_gather(share, 'dev', axis=0, tiled=True)]
    all_to_all x4 -> x0, waiting for transfers between devices: 45.7 us -> none  [the longest x1 45.7 us: on_device(): lax.all_to_all(grads_four, 'grp', split_axis=0, concat_axis=0, tiled=True)]
    scatter x2 -> x0, local copies, waits for them, and re-layouts: 28.8 us -> none  [the longest x1 15.7 us: pack_cold(): jnp.zeros((devices * slots,), jnp.int32).at[target].set(cold_row)]
    reduce_scatter x1 -> x0, waiting for transfers between devices: 28.5 us -> none  [hot_update(): lax.psum_scatter(partial_sum, 'dev', scatter_dimension=0, tiled=True)]
    all_to_all x4 -> x0, starting transfers between devices: 20.8 us -> none  [the longest x1 6.7 us: on_device(): lax.all_to_all(lax.all_to_all(rows_three, 'grp', split_axis=0, concat_axi...]
    psum x1 -> x0, blocking collectives: 11.9 us -> none  [hot_update(): share = lax.psum(share, 'grp')]
  transfers between devices with their start and end apart: 5 -> 0, of which waited for: 2 -> 0; matrix products, arithmetic and copies ran while one was open for 9% -> 0% of each run, Pallas kernels for 0% -> 0%
where the time goes in v1:
time: 162 us; the launch traced here: 159 us
  Pallas kernels  150 us (93%)
  local copies, waits for them, and re-layouts  9.1 us (6%)
    pallas_call x1, Pallas kernels, on_device(): pl.pallas_call(functools.partial(exchange_kernel, n_grp, n_dev), out_shap...  108 us
    pallas_call x1, Pallas kernels, on_device(): pl.pallas_call(functools.partial(apply_kernel, slots), out_shape=jax.Shap...  24 us
    pallas_call x1, Pallas kernels, on_device(): pl.pallas_call(pack_kernel, out_shape=(jax.ShapeDtypeStruct((devices * sl...  11.3 us
    unnamed x12, local copies, waits for them, and re-layouts  7.47 us
    pallas_call x1, Pallas kernels, on_device(): pl.pallas_call(functools.partial(plan_kernel, slots), out_shape=(jax.Shap...  6.64 us

profile of v1, /device:TPU:13, one launch (start us, length us, event | category | flops | bytes accessed | tf_op | source)
XLA Modules:
  0.0 159.1 jit_solution(14418805616318606973)
XLA Ops:
  0.0 2.7 %copy.8.owner_ref = s32[4096,1]{1,0:T(8,128)} copy(s32[4096,1]{0,1:T(1,128)} %param.9) | data formatting | bytes 32768 | tf_op args[2]
  2.7 6.6 %plan.1 = (s32[32,128]{1,0:T(8,128)}, s32[8,128]{1,0:T(8,128)}, f32[256,128]{1,0:T(8,128)}) custom-call(s32[4096,1]{1,0:T(8,128)} %copy.8.owner_ref, f32[1024,128]{1,0:T(8,128)} %hot_grads_ref.1, s32[1,1024]{1,0:T(1,128)} %bitcast.28), custom_call_target="tpu_custom_call" | custom-call | tf_op jit(solution)/shard_map/plan/pallas_call | solution.py:213
  9.3 0.0 copy-start.2
  9.3 11.3 %pack.1 = (f32[8192,128]{1,0:T(8,128)}, s32[8192]{0:T(1024)}) custom-call(s32[4096]{0:T(1024)} %bitcast.27, s32[4096]{0:T(1024)} %row_ref.1, f32[4096,128]{1,0:T(8,128)} %grads_ref.1), custom_call_target="tpu_custom_call" | custom-call | tf_op jit(solution)/shard_map/pack/pallas_call | solution.py:224
  20.6 0.8 reshape.30
  21.4 0.7 slice_bitcast_fusion.1
  22.1 0.1 copy.9
  22.2 0.1 pad.2.clone
  22.3 0.7 copy.12
  23.0 107.9 %exchange.1 = (f32[32,256,128]{2,1,0:T(8,128)}, s32[32,8,128]{2,1,0:T(8,128)}, f32[32,8,128]{2,1,0:T(8,128)}) custom-call(f32[32,256,128]{2,1,0:T(8,128)} %bitcast.21, s32[32,8,128]{2,1,0:T(8,128)} %bitcast.22, f32[32,8,128]{2,1,0:T(8,128)} %bitcast.25), custom_call_target="tpu_custom_call" | custom-call | tf_op jit(solution)/shard_map/exchange/pallas_call | solution.py:242
  130.9 0.9 copy.16
  131.9 0.1 copy.11
  132.0 0.0 copy-done.2
  132.0 0.0 copy-start
  132.0 2.2 %copy-done = f32[8192,128]{1,0:T(8,128)S(1)} copy-done((f32[8192,128]{1,0:T(8,128)S(1)}, f32[8192,128]{1,0:T(8,128)}, u32[]{:S(2)}) %copy-start) | copy-done | bytes 4194328
  134.2 0.0 copy-start.1
  134.2 0.9 copy-done.1
  135.1 24.0 %apply.1 = f32[8192,128]{1,0:T(8,128)} custom-call(s32[8192]{0:T(1024)S(1)} %bitcast.19, s32[32]{0:T(128)S(1)} %bitcast.20, s32[256]{0:T(256)S(1)} %broadcast_subtract_fusion.local_ref, f32[8192,128]{1,0:T(8,128)S(1)} %copy-done, f32[32,256,128]{2,1,0:T(8,128)} %get-tuple-element.19.got_ref, f32[256,128]{1,0:T(8,128)S(1)} %bitcast.18), custom_call_target="tpu_custom_call" | custom-call | tf_op jit(solution)/shard_map/apply/pallas_call | solution.py:257
  (6 shorter events, 0.0 us)
Async XLA Ops:
  9.3 122.6 %copy-start.2 = (s32[256]{0:T(256)S(1)}, s32[256]{0:T(256)}, u32[]{:S(2)}) copy-start(s32[256]{0:T(256)} %param.13) | copy-start | bytes 3076
  132.0 2.2 %copy-start = (f32[8192,128]{1,0:T(8,128)S(1)}, f32[8192,128]{1,0:T(8,128)}, u32[]{:S(2)}) copy-start(f32[8192,128]{1,0:T(8,128)} %table_ref.1) | copy-start | bytes 12582916
  134.2 0.9 copy-start.1

commit v2 on v1

v2 whole, which is shorter than its diff:
```python
import functools

import jax
import jax.numpy as jnp
from jax import lax
from jax.experimental import pallas as pl
from jax.experimental.pallas import tpu as pltpu
from jax.sharding import PartitionSpec as P

LEARN = 0.05
MESH = pl.DeviceIdType.MESH
LANES = 128
CHUNK = 256


def plan_kernel(slots, owner_ref, hot_grads_ref, hot_slot_ref, place_ref, count_ref, partial_ref):
    lookups = owner_ref.shape[0]
    wide = count_ref.shape[1]
    above = lax.broadcasted_iota(jnp.int32, (CHUNK, CHUNK), 0)
    below = lax.broadcasted_iota(jnp.int32, (CHUNK, CHUNK), 1)
    tri = (above >= below).astype(jnp.bfloat16)
    owners = lax.broadcasted_iota(jnp.int32, (CHUNK, wide), 1)
    start = owners.astype(jnp.float32) * slots - 1.0
    ones = jnp.ones((8, wide), jnp.float32)
    base = jnp.zeros((1, wide), jnp.float32)
    for b in range(lookups // CHUNK):
        hit = owner_ref[b * CHUNK:(b + 1) * CHUNK, :] == owners
        run = jnp.dot(tri, hit.astype(jnp.bfloat16), preferred_element_type=jnp.float32) + base
        base = run[CHUNK - 1:CHUNK, :]
        chosen = jnp.where(hit, run + start, 0.0)
        flat = lax.dot_general(
            ones, chosen, (((1,), (1,)), ((), ())),
            precision=lax.Precision.HIGHEST, preferred_element_type=jnp.float32,
        )
        whole = (flat + 0.5).astype(jnp.int32)
        for j in range(CHUNK // LANES):
            r = b * (CHUNK // LANES) + j
            place_ref[r:r + 1, :] = whole[0:1, j * LANES:(j + 1) * LANES]
    count_ref[...] = jnp.broadcast_to((base + 0.5).astype(jnp.int32), count_ref.shape)
    hot = partial_ref.shape[0]
    looks = hot_grads_ref.shape[0]
    pick = lax.broadcasted_iota(jnp.int32, (hot, looks), 0) == hot_slot_ref[...]
    partial_ref[...] = jnp.dot(
        pick.astype(jnp.float32), hot_grads_ref[...],
        precision=lax.Precision.HIGHEST, preferred_element_type=jnp.float32,
    )


def pack_kernel(place_ref, row_ref, grads_ref, send_ref, rows_ref):
    step = 16

    def body(t, carry):
        first = pl.multiple_of(t * step, step)
        for j in range(step):
            to = place_ref[first + j]
            rows_ref[to] = row_ref[first + j]
            send_ref[pl.ds(to, 1), :] = grads_ref[pl.ds(first + j, 1), :]
        return carry

    lax.fori_loop(0, grads_ref.shape[0] // step, body, 0)


def exchange_kernel(
    n_grp, n_dev, slots, send_ref, meta_ref, part_ref, local_ref, table_ref, out_ref,
    got, gmeta, total, rbuf, acc, halves, s_big, r_big, s_meta, r_meta, s_rs, r_rs, s_ag, r_ag, s_own,
):
    devices = n_grp * n_dev
    width = acc.shape[1]
    rows_dev = acc.shape[0]
    tile = min(1024, rows_dev)
    me = lax.axis_index("grp") * n_dev + lax.axis_index("dev")
    barrier = pltpu.get_barrier_semaphore()

    def each(fn, first=1, last=devices):
        def body(k, carry):
            p = lax.rem(me + k, devices)
            fn(k, p, (p // n_dev, lax.rem(p, n_dev)))
            return carry
        lax.fori_loop(first, last, body, 0)

    def remote(src, dst, ssem, rsem, where):
        return pltpu.make_async_remote_copy(
            src_ref=src, dst_ref=dst, send_sem=ssem, recv_sem=rsem,
            device_id=where, device_id_type=MESH,
        )

    load = pltpu.make_async_copy(table_ref, acc, s_own.at[0])
    load.start()
    own_big = pltpu.make_async_copy(send_ref.at[me], got.at[me], s_own.at[1])
    own_big.start()
    each(lambda k, p, w: pl.semaphore_signal(barrier, inc=1, device_id=w, device_id_type=MESH))
    pl.semaphore_wait(barrier, devices - 1)

    def big(k, p, w):
        remote(send_ref.at[p], got.at[me], s_big, r_big.at[k], w).start()

    half = devices // 2
    each(lambda k, p, w: remote(part_ref.at[p], rbuf.at[me], s_rs, r_rs, w).start())
    each(lambda k, p, w: remote(meta_ref.at[p], gmeta.at[me], s_meta, r_meta, w).start())
    each(big, 1, half)
    rbuf[me] = part_ref[me]
    gmeta[me] = meta_ref[me]

    here = (lax.axis_index("grp"), lax.axis_index("dev"))
    most = pl.ds(0, devices - 1)

    def all_of(src, dst, ssem, rsem):
        return remote(src.at[most], dst.at[most], ssem, rsem, here)

    rs = all_of(part_ref, rbuf, s_rs, r_rs)
    rs.wait_recv()
    total[me] = jnp.sum(rbuf[...], axis=0)
    each(big, half, half + half // 2)
    rs.wait_send()
    each(lambda k, p, w: remote(total.at[me], total.at[me], s_ag, r_ag, w).start())
    each(big, half + half // 2, devices)

    def add(values, ids):
        count = values.shape[0]
        high = values.astype(jnp.bfloat16)
        halves[0:count, 0:width] = high
        halves[0:count, width:2 * width] = (values - high.astype(jnp.float32)).astype(jnp.bfloat16)
        spot = lax.broadcasted_iota(jnp.int32, (tile, count), 0)

        def body(t, carry):
            at = pl.multiple_of(t * tile, tile)
            hit = jnp.where(spot == ids - at, 1.0, 0.0).astype(jnp.bfloat16)
            both = jnp.dot(hit, halves[0:count, :], preferred_element_type=jnp.float32)
            w = pl.ds(at, tile)
            acc[w, :] = acc[w, :] - LEARN * (both[:, :width] + both[:, width:])
            return carry

        lax.fori_loop(0, rows_dev // tile, body, 0)

    lines = -(-slots // LANES)

    def add_block(source):
        info = gmeta[source]
        filled = info[lines:lines + 1, :]
        ids = jnp.concatenate([info[j:j + 1, :] for j in range(lines)], axis=1)[:, :slots]
        held = jnp.concatenate([filled] * lines, axis=1)[:, :slots]
        ids = jnp.where(lax.broadcasted_iota(jnp.int32, (1, slots), 1) < held, ids, -1)
        block = got[source]
        deep = lax.broadcasted_iota(jnp.int32, block.shape, 0)
        add(jnp.where(deep < filled[:, :width], block, 0.0), ids)

    load.wait()
    own_big.wait()
    add_block(me)
    metas = all_of(meta_ref, gmeta, s_meta, r_meta)
    metas.wait_send()
    metas.wait_recv()

    def arrived(k, carry):
        source = lax.rem(me - k + devices, devices)
        remote(send_ref.at[0], got.at[source], s_big, r_big.at[k], here).wait_recv()
        add_block(source)
        return carry

    lax.fori_loop(1, devices, arrived, 0)
    ag = all_of(total, total, s_ag, r_ag)
    ag.wait_send()
    ag.wait_recv()
    hot = local_ref.shape[1]
    add(total[...].reshape(-1, width)[:hot], local_ref[...])
    out = pltpu.make_async_copy(acc, out_ref, s_own.at[0])
    out.start()
    remote(send_ref.at[most], got.at[most], s_big, r_big.at[0], here).wait_send()
    out.wait()


def on_device(n_grp, n_dev, table, cold_grads, cold_owner, cold_row, hot_grads, hot_slot, hot_ids):
    devices = n_grp * n_dev
    width = table.shape[1]
    lookups = cold_grads.shape[0]
    rows_dev = table.shape[0]
    hot = hot_ids.shape[0]
    slots = max(4, 2 * lookups // devices)
    wide = -(-devices // LANES) * LANES
    vmem, smem, hbm = (pl.BlockSpec(memory_space=m) for m in (pltpu.VMEM, pltpu.SMEM, pl.ANY))
    f32, i32 = jnp.float32, jnp.int32
    place, count, partial = pl.pallas_call(
        functools.partial(plan_kernel, slots),
        out_shape=(
            jax.ShapeDtypeStruct((lookups // LANES, LANES), i32),
            jax.ShapeDtypeStruct((8, wide), i32),
            jax.ShapeDtypeStruct((hot, width), f32),
        ),
        in_specs=[vmem] * 3,
        out_specs=(vmem,) * 3,
        name="plan",
    )(cold_owner, hot_grads, hot_slot.reshape(1, -1))
    send, rows = pl.pallas_call(
        pack_kernel,
        out_shape=(
            jax.ShapeDtypeStruct((devices * slots, width), f32),
            jax.ShapeDtypeStruct((devices * slots,), i32),
        ),
        in_specs=[smem, smem, vmem],
        out_specs=(vmem, smem),
        name="pack",
    )(place.reshape(-1), cold_row, cold_grads)
    lines = -(-slots // LANES)
    rows = jnp.pad(rows.reshape(devices, slots), ((0, 0), (0, lines * LANES - slots)))
    height = -(-(lines + 1) // 8) * 8
    meta = jnp.concatenate(
        [rows.reshape(devices, lines, LANES),
         jnp.broadcast_to(count[0, :devices, None, None], (devices, height - lines, LANES))], axis=1,
    )
    share = -(-hot // devices)
    partial = jnp.pad(partial, ((0, share * devices - hot), (0, 0))).reshape(devices, share, width)
    me = lax.axis_index("grp") * n_dev + lax.axis_index("dev")
    dma = pltpu.SemaphoreType.DMA
    return pl.pallas_call(
        functools.partial(exchange_kernel, n_grp, n_dev, slots),
        out_shape=jax.ShapeDtypeStruct(table.shape, f32),
        in_specs=[hbm, vmem, vmem, vmem, hbm],
        out_specs=hbm,
        scratch_shapes=[
            pltpu.VMEM((devices, slots, width), f32),
            pltpu.VMEM(meta.shape, i32),
            pltpu.VMEM(partial.shape, f32),
            pltpu.VMEM(partial.shape, f32),
            pltpu.VMEM(table.shape, f32),
            pltpu.VMEM((max(slots, hot), 2 * width), jnp.bfloat16),
            dma, dma((devices,)), dma, dma, dma, dma, dma, dma, dma((2,)),
        ],
        compiler_params=pltpu.CompilerParams(
            collective_id=0, has_side_effects=True, vmem_limit_bytes=48 * 1024 * 1024
        ),
        name="exchange",
    )(send.reshape(devices, slots, width), meta, partial,
      (hot_ids - me * rows_dev).reshape(1, -1), table)


def solution(mesh):
    in_specs = (
        P(("grp", "dev"), None),
        P(("grp", "dev"), None),
        P(("grp", "dev"), None),
        P(("grp", "dev")),
        P(("grp", "dev"), None),
        P(("grp", "dev")),
        P(),
    )
    out_specs = P(("grp", "dev"), None)
    return jax.shard_map(
        functools.partial(on_device, mesh.shape["grp"], mesh.shape["dev"]),
        mesh=mesh, in_specs=in_specs, out_specs=out_specs, check_vma=False,
    )
```

time: 162 us -> 158 us (0.975)
  local copies, waits for them, and re-layouts: 9.1 us -> 6.36 us
  Pallas kernels: 150 us -> 148 us
    unnamed x12 -> x4, local copies, waits for them, and re-layouts: 7.47 us -> 5.59 us
    pallas_call x2 -> x1, Pallas kernels: 132 us -> 130 us  [on_device(): pl.pallas_call(functools.partial(exchange_kernel, n_grp, n_dev, slots), o...]
where the time goes in v2:
time: 158 us; the launch traced here: 156 us
  Pallas kernels  148 us (94%)
  local copies, waits for them, and re-layouts  6.36 us (4%)
    pallas_call x1, Pallas kernels, on_device(): pl.pallas_call(functools.partial(exchange_kernel, n_grp, n_dev, slots), o...  130 us
    pallas_call x1, Pallas kernels, on_device(): pl.pallas_call(pack_kernel, out_shape=(jax.ShapeDtypeStruct((devices * sl...  11.3 us
    pallas_call x1, Pallas kernels, on_device(): pl.pallas_call(functools.partial(plan_kernel, slots), out_shape=(jax.Shap...  6.65 us
    unnamed x4, local copies, waits for them, and re-layouts  5.59 us

profile of v2, /device:TPU:13, one launch (start us, length us, event | category | flops | bytes accessed | tf_op | source)
XLA Modules:
  0.0 156.0 jit_solution(5645955878323418667)
XLA Ops:
  0.0 0.7 broadcast_subtract_fusion
  0.7 2.7 %copy.8.owner_ref = s32[4096,1]{1,0:T(8,128)} copy(s32[4096,1]{0,1:T(1,128)} %param.9) | data formatting | bytes 32768 | tf_op args[2]
  3.4 6.7 %plan.1 = (s32[32,128]{1,0:T(8,128)}, s32[8,128]{1,0:T(8,128)}, f32[256,128]{1,0:T(8,128)}) custom-call(s32[4096,1]{1,0:T(8,128)} %copy.8.owner_ref, f32[1024,128]{1,0:T(8,128)} %hot_grads_ref.1, s32[1,1024]{1,0:T(1,128)} %bitcast.13), custom_call_target="tpu_custom_call" | custom-call | tf_op jit(solution)/shard_map/plan/pallas_call | solution.py:182
  10.0 0.7 slice_bitcast_fusion
  10.7 0.1 broadcast_in_dim.8
  10.8 11.3 %pack.1 = (f32[8192,128]{1,0:T(8,128)}, s32[8192]{0:T(1024)}) custom-call(s32[4096]{0:T(1024)} %bitcast.12, s32[4096]{0:T(1024)} %row_ref.1, f32[4096,128]{1,0:T(8,128)} %grads_ref.1), custom_call_target="tpu_custom_call" | custom-call | tf_op jit(solution)/shard_map/pack/pallas_call | solution.py:193
  22.1 0.8 pad_add_fusion.meta_ref
  22.9 0.0 copy-start
  22.9 0.9 copy-done
  23.8 130.1 %exchange.1 = f32[8192,128]{1,0:T(8,128)S(1)} custom-call(f32[32,256,128]{2,1,0:T(8,128)} %bitcast.10, s32[32,8,128]{2,1,0:T(8,128)S(1)} %pad_add_fusion.meta_ref, f32[32,8,128]{2,1,0:T(8,128)S(1)} %bitcast.8, s32[1,256]{1,0:T(1,128)S(1)} %bitcast.9, f32[8192,128]{1,0:T(8,128)} %table_ref.1), custom_call_target="tpu_custom_call" | custom-call | tf_op jit(solution)/shard_map/exchange/pallas_call | solution.py:214
  154.0 2.0 %copy.10 = f32[8192,128]{1,0:T(8,128)} copy(f32[8192,128]{1,0:T(8,128)S(1)} %exchange.1) | data formatting | bytes 8388608
Async XLA Ops:
  22.9 0.9 copy-start

commit v3 on v2

--- a/solution.py
+++ b/solution.py
@@ -11,39 +11,45 @@
 MESH = pl.DeviceIdType.MESH
 LANES = 128
 CHUNK = 256
+MIB = 1024 * 1024
+TILE = 4096
+
+
+def parts_of(values):
+    high = values.astype(jnp.bfloat16)
+    rest = values - high.astype(jnp.float32)
+    middle = rest.astype(jnp.bfloat16)
+    low = (rest - middle.astype(jnp.float32)).astype(jnp.bfloat16)
+    return high, middle, low
 
 
 def plan_kernel(slots, owner_ref, hot_grads_ref, hot_slot_ref, place_ref, count_ref, partial_ref):
-    lookups = owner_ref.shape[0]
-    wide = count_ref.shape[1]
-    above = lax.broadcasted_iota(jnp.int32, (CHUNK, CHUNK), 0)
-    below = lax.broadcasted_iota(jnp.int32, (CHUNK, CHUNK), 1)
-    tri = (above >= below).astype(jnp.bfloat16)
-    owners = lax.broadcasted_iota(jnp.int32, (CHUNK, wide), 1)
-    start = owners.astype(jnp.float32) * slots - 1.0
-    ones = jnp.ones((8, wide), jnp.float32)
-    base = jnp.zeros((1, wide), jnp.float32)
-    for b in range(lookups // CHUNK):
-        hit = owner_ref[b * CHUNK:(b + 1) * CHUNK, :] == owners
-        run = jnp.dot(tri, hit.astype(jnp.bfloat16), preferred_element_type=jnp.float32) + base
-        base = run[CHUNK - 1:CHUNK, :]
-        chosen = jnp.where(hit, run + start, 0.0)
-        flat = lax.dot_general(
-            ones, chosen, (((1,), (1,)), ((), ())),
-            precision=lax.Precision.HIGHEST, preferred_element_type=jnp.float32,
-        )
-        whole = (flat + 0.5).astype(jnp.int32)
-        for j in range(CHUNK // LANES):
-            r = b * (CHUNK // LANES) + j
-            place_ref[r:r + 1, :] = whole[0:1, j * LANES:(j + 1) * LANES]
-    count_ref[...] = jnp.broadcast_to((base + 0.5).astype(jnp.int32), count_ref.shape)
-    hot = partial_ref.shape[0]
+    blocks = owner_ref.shape[0] * LANES // CHUNK
+    lines = CHUNK // LANES
+    tall = count_ref.shape[0]
+    before = lax.broadcasted_iota(jnp.int32, (CHUNK, CHUNK), 0)
+    after = lax.broadcasted_iota(jnp.int32, (CHUNK, CHUNK), 1)
+    tri = (before <= after).astype(jnp.bfloat16)
+    owners = lax.broadcasted_iota(jnp.int32, (tall, CHUNK), 0)
+    base = owners.astype(jnp.float32)[:, 0:1] * slots - 1.0
+    start = base
+    for b in range(blocks):
+        own = jnp.concatenate([owner_ref[b * lines + j:b * lines + j + 1, :] for j in range(lines)], axis=1)
+        hit = own == owners
+        run = jnp.dot(hit.astype(jnp.bfloat16), tri, preferred_element_type=jnp.float32) + base
+        base = run[:, CHUNK - 1:CHUNK]
+        spot = jnp.sum(jnp.where(hit, run, 0.0), axis=0, keepdims=True)
+        whole = (spot + 0.5).astype(jnp.int32)
+        for j in range(lines):
+            r = b * lines + j
+            place_ref[r:r + 1, :] = whole[:, j * LANES:(j + 1) * LANES]
+    count_ref[...] = jnp.broadcast_to((base - start + 0.5).astype(jnp.int32), count_ref.shape)
+    hot, width = partial_ref.shape
     looks = hot_grads_ref.shape[0]
     pick = lax.broadcasted_iota(jnp.int32, (hot, looks), 0) == hot_slot_ref[...]
-    partial_ref[...] = jnp.dot(
-        pick.astype(jnp.float32), hot_grads_ref[...],
-        precision=lax.Precision.HIGHEST, preferred_element_type=jnp.float32,
-    )
+    split = jnp.concatenate(parts_of(hot_grads_ref[...]), axis=1)
+    three = jnp.dot(pick.astype(jnp.bfloat16), split, preferred_element_type=jnp.float32)
+    partial_ref[...] = three[:, :width] + three[:, width:2 * width] + three[:, 2 * width:]
 
 
 def pack_kernel(place_ref, row_ref, grads_ref, send_ref, rows_ref):
@@ -61,13 +67,13 @@
 
 
 def exchange_kernel(
-    n_grp, n_dev, slots, send_ref, meta_ref, part_ref, local_ref, table_ref, out_ref,
+    n_grp, n_dev, slots, send_ref, meta_ref, part_ref, ids_ref, table_ref, out_ref,
     got, gmeta, total, rbuf, acc, halves, s_big, r_big, s_meta, r_meta, s_rs, r_rs, s_ag, r_ag, s_own,
 ):
     devices = n_grp * n_dev
     width = acc.shape[1]
     rows_dev = acc.shape[0]
-    tile = min(1024, rows_dev)
+    tile = min(TILE, rows_dev)
     me = lax.axis_index("grp") * n_dev + lax.axis_index("dev")
     barrier = pltpu.get_barrier_semaphore()
 
@@ -161,8 +167,8 @@
     ag = all_of(total, total, s_ag, r_ag)
     ag.wait_send()
     ag.wait_recv()
-    hot = local_ref.shape[1]
-    add(total[...].reshape(-1, width)[:hot], local_ref[...])
+    hot = ids_ref.shape[1]
+    add(total[...].reshape(-1, width)[:hot], ids_ref[...] - me * rows_dev)
     out = pltpu.make_async_copy(acc, out_ref, s_own.at[0])
     out.start()
     remote(send_ref.at[most], got.at[most], s_big, r_big.at[0], here).wait_send()
@@ -176,20 +182,21 @@
     rows_dev = table.shape[0]
     hot = hot_ids.shape[0]
     slots = max(4, 2 * lookups // devices)
-    wide = -(-devices // LANES) * LANES
+    tall = -(-devices // 8) * 8
     vmem, smem, hbm = (pl.BlockSpec(memory_space=m) for m in (pltpu.VMEM, pltpu.SMEM, pl.ANY))
     f32, i32 = jnp.float32, jnp.int32
     place, count, partial = pl.pallas_call(
         functools.partial(plan_kernel, slots),
         out_shape=(
             jax.ShapeDtypeStruct((lookups // LANES, LANES), i32),
-            jax.ShapeDtypeStruct((8, wide), i32),
+            jax.ShapeDtypeStruct((tall, LANES), i32),
             jax.ShapeDtypeStruct((hot, width), f32),
         ),
         in_specs=[vmem] * 3,
         out_specs=(vmem,) * 3,
+        compiler_params=pltpu.CompilerParams(vmem_limit_bytes=8 * MIB),
         name="plan",
-    )(cold_owner, hot_grads, hot_slot.reshape(1, -1))
+    )(cold_owner.reshape(-1, LANES), hot_grads, hot_slot.reshape(1, -1))
     send, rows = pl.pallas_call(
         pack_kernel,
         out_shape=(
@@ -198,6 +205,7 @@
         ),
         in_specs=[smem, smem, vmem],
         out_specs=(vmem, smem),
+        compiler_params=pltpu.CompilerParams(vmem_limit_bytes=12 * MIB),
         name="pack",
     )(place.reshape(-1), cold_row, cold_grads)
     lines = -(-slots // LANES)
@@ -205,11 +213,10 @@
     height = -(-(lines + 1) // 8) * 8
     meta = jnp.concatenate(
         [rows.reshape(devices, lines, LANES),
-         jnp.broadcast_to(count[0, :devices, None, None], (devices, height - lines, LANES))], axis=1,
+         jnp.broadcast_to(count[:devices, None, :], (devices, height - lines, LANES))], axis=1,
     )
     share = -(-hot // devices)
     partial = jnp.pad(partial, ((0, share * devices - hot), (0, 0))).reshape(devices, share, width)
-    me = lax.axis_index("grp") * n_dev + lax.axis_index("dev")
     dma = pltpu.SemaphoreType.DMA
     return pl.pallas_call(
         functools.partial(exchange_kernel, n_grp, n_dev, slots),
@@ -226,11 +233,11 @@
             dma, dma((devices,)), dma, dma, dma, dma, dma, dma, dma((2,)),
         ],
         compiler_params=pltpu.CompilerParams(
-            collective_id=0, has_side_effects=True, vmem_limit_bytes=48 * 1024 * 1024
+            collective_id=0, has_side_effects=True, vmem_limit_bytes=32 * MIB
         ),
         name="exchange",
     )(send.reshape(devices, slots, width), meta, partial,
-      (hot_ids - me * rows_dev).reshape(1, -1), table)
+      hot_ids.reshape(1, -1), table)
 
 
 def solution(mesh):

time: 158 us -> 133 us (0.84)
  Pallas kernels: 148 us -> 123 us
  local copies, waits for them, and re-layouts: 6.36 us -> 9.63 us
    pallas_call x1, Pallas kernels: 130 us -> 112 us  [on_device(): pl.pallas_call(functools.partial(exchange_kernel, n_grp, n_dev, slots), o...]
    pallas_call x1, Pallas kernels: 6.65 us -> 1.27 us  [on_device(): pl.pallas_call(functools.partial(plan_kernel, slots), out_shape=(jax.Shap...]
    unnamed x4 -> x15, local copies, waits for them, and re-layouts: 5.59 us -> 9.62 us
    pallas_call x1, Pallas kernels: 11.3 us -> 9.6 us  [on_device(): pl.pallas_call(pack_kernel, out_shape=(jax.ShapeDtypeStruct((devices * sl...]
where the time goes in v3:
time: 133 us; the launch traced here: 132 us
  Pallas kernels  123 us (92%)
  local copies, waits for them, and re-layouts  9.63 us (7%)
    pallas_call x1, Pallas kernels, on_device(): pl.pallas_call(functools.partial(exchange_kernel, n_grp, n_dev, slots), o...  112 us
    unnamed x15, local copies, waits for them, and re-layouts  9.62 us
    pallas_call x1, Pallas kernels, on_device(): pl.pallas_call(pack_kernel, out_shape=(jax.ShapeDtypeStruct((devices * sl...  9.6 us

profile of v3, /device:TPU:13, one launch (start us, length us, event | category | flops | bytes accessed | tf_op | source)
XLA Modules:
  0.0 132.5 jit_solution(3611728212942842803)
XLA Ops:
  0.0 0.0 copy-start.2
  0.0 1.0 copy-done.2
  1.0 0.0 copy-start.4
  1.0 0.7 copy-done.4
  1.8 0.0 copy-start.5
  1.8 0.7 copy-done.5
  2.4 1.3 plan.1
  3.7 0.0 copy-start.1
  3.7 1.6 %copy-done.1 = f32[4096,128]{1,0:T(8,128)S(1)} copy-done((f32[4096,128]{1,0:T(8,128)S(1)}, f32[4096,128]{1,0:T(8,128)}, u32[]{:S(2)}) %copy-start.1) | copy-done | bytes 2097176
  5.3 0.0 copy-start.3
  5.3 0.7 copy-done.3
  6.0 9.6 %pack.1 = (f32[8192,128]{1,0:T(8,128)S(1)}, s32[8192]{0:T(1024)S(1)}) custom-call(s32[4096]{0:T(1024)S(1)} %bitcast.10, s32[4096]{0:T(1024)S(1)} %copy-done.3, f32[4096,128]{1,0:T(8,128)S(1)} %copy-done.1), custom_call_target="tpu_custom_call" | custom-call | tf_op jit(solution)/shard_map/pack/pallas_call | solution.py:200
  15.7 0.0 copy-start
  15.7 2.2 %copy-done = f32[8192,128]{1,0:T(8,128)S(1)} copy-done((f32[8192,128]{1,0:T(8,128)S(1)}, f32[8192,128]{1,0:T(8,128)}, u32[]{:S(2)}) %copy-start) | copy-done | bytes 4194328
  17.9 0.0 copy-start.6
  17.9 0.7 copy-done.6
  18.6 111.9 %exchange.1 = f32[8192,128]{1,0:T(8,128)S(1)} custom-call(f32[32,256,128]{2,1,0:T(8,128)S(1)} %bitcast.7, s32[32,8,128]{2,1,0:T(8,128)S(1)} %pad_add_fusion.meta_ref, f32[32,8,128]{2,1,0:T(8,128)S(1)} %bitcast.8, s32[1,256]{1,0:T(1,128)S(1)} %bitcast.13, f32[8192,128]{1,0:T(8,128)S(1)} %copy-done), custom_call_target="tpu_custom_call" | custom-call | tf_op jit(solution)/shard_map/exchange/pallas_call | solution.py:221
  130.5 2.0 %copy.9 = f32[8192,128]{1,0:T(8,128)} copy(f32[8192,128]{1,0:T(8,128)S(1)} %exchange.1) | data formatting | bytes 8388608
  (2 shorter events, 0.0 us)
Async XLA Ops:
  0.0 1.0 copy-start.2
  1.0 0.7 copy-start.4
  1.8 0.7 copy-start.5
  3.7 1.6 %copy-start.1 = (f32[4096,128]{1,0:T(8,128)S(1)}, f32[4096,128]{1,0:T(8,128)}, u32[]{:S(2)}) copy-start(f32[4096,128]{1,0:T(8,128)} %grads_ref.1) | copy-start | bytes 6291460
  5.3 0.7 copy-start.3
  15.7 2.2 %copy-start = (f32[8192,128]{1,0:T(8,128)S(1)}, f32[8192,128]{1,0:T(8,128)}, u32[]{:S(2)}) copy-start(f32[8192,128]{1,0:T(8,128)} %table_ref.1) | copy-start | bytes 12582916
  17.9 0.7 copy-start.6

commit v4 on v3

--- a/solution.py
+++ b/solution.py
@@ -11,6 +11,7 @@
 MESH = pl.DeviceIdType.MESH
 LANES = 128
 CHUNK = 256
+STEP = 16
 MIB = 1024 * 1024
 TILE = 4096
 
@@ -23,7 +24,21 @@
     return high, middle, low
 
 
-def plan_kernel(slots, owner_ref, hot_grads_ref, hot_slot_ref, place_ref, count_ref, partial_ref):
+def pack_kernel(
+    slots, owner_hbm, row_hbm, grads_hbm, hot_grads_hbm, hot_slot_hbm,
+    send_ref, rows_ref, count_ref, partial_ref,
+    owner_ref, row_ref, grads_ref, hot_grads_ref, hot_slot_ref, place_ref, place_smem, sem,
+):
+    copies = [
+        pltpu.make_async_copy(a, b, sem.at[i])
+        for i, (a, b) in enumerate([
+            (owner_hbm, owner_ref), (row_hbm, row_ref), (grads_hbm, grads_ref),
+            (hot_grads_hbm, hot_grads_ref), (hot_slot_hbm, hot_slot_ref),
+        ])
+    ]
+    for c in copies:
+        c.start()
+    copies[0].wait()
     blocks = owner_ref.shape[0] * LANES // CHUNK
     lines = CHUNK // LANES
     tall = count_ref.shape[0]
@@ -43,44 +58,63 @@
         for j in range(lines):
             r = b * lines + j
             place_ref[r:r + 1, :] = whole[:, j * LANES:(j + 1) * LANES]
+    placed = pltpu.make_async_copy(place_ref, place_smem, sem.at[5])
+    placed.start()
     count_ref[...] = jnp.broadcast_to((base - start + 0.5).astype(jnp.int32), count_ref.shape)
+    copies[3].wait()
+    copies[4].wait()
     hot, width = partial_ref.shape
     looks = hot_grads_ref.shape[0]
     pick = lax.broadcasted_iota(jnp.int32, (hot, looks), 0) == hot_slot_ref[...]
     split = jnp.concatenate(parts_of(hot_grads_ref[...]), axis=1)
     three = jnp.dot(pick.astype(jnp.bfloat16), split, preferred_element_type=jnp.float32)
     partial_ref[...] = three[:, :width] + three[:, width:2 * width] + three[:, 2 * width:]
-
-
-def pack_kernel(place_ref, row_ref, grads_ref, send_ref, rows_ref):
-    step = 16
-
-    def body(t, carry):
-        first = pl.multiple_of(t * step, step)
-        for j in range(step):
-            to = place_ref[first + j]
-            rows_ref[to] = row_ref[first + j]
-            send_ref[pl.ds(to, 1), :] = grads_ref[pl.ds(first + j, 1), :]
-        return carry
-
-    lax.fori_loop(0, grads_ref.shape[0] // step, body, 0)
+    copies[1].wait()
+    copies[2].wait()
+    placed.wait()
+
+    def body(line, carry):
+        def part(q, c):
+            first = pl.multiple_of(q * STEP, STEP)
+            for j in range(STEP):
+                to = place_smem[line, first + j]
+                at = line * LANES + first + j
+                rows_ref[to] = row_ref[at]
+                send_ref[pl.ds(to, 1), :] = grads_ref[pl.ds(at, 1), :]
+            return c
+
+        return lax.fori_loop(0, LANES // STEP, part, carry)
+
+    lax.fori_loop(0, place_ref.shape[0], body, 0)
+
+
+def partner(at, step, size):
+    if size & (size - 1):
+        return lax.rem(at + step, size), lax.rem(at - step + size, size)
+    mixed = 0
+    bit = 1
+    while bit < size:
+        mixed = mixed + bit * lax.rem(at // bit + step // bit, 2)
+        bit *= 2
+    return mixed, mixed
 
 
 def exchange_kernel(
-    n_grp, n_dev, slots, send_ref, meta_ref, part_ref, ids_ref, table_ref, out_ref,
-    got, gmeta, total, rbuf, acc, halves, s_big, r_big, s_meta, r_meta, s_rs, r_rs, s_ag, r_ag, s_own,
+    n_grp, n_dev, slots, send_ref, meta_ref, part_ref, ids_ref, table_ref, acc,
+    got, gmeta, total, rbuf, halves, s_big, r_big, s_meta, r_meta, s_rs, r_rs, s_ag, r_ag, s_own,
 ):
     devices = n_grp * n_dev
     width = acc.shape[1]
     rows_dev = acc.shape[0]
     tile = min(TILE, rows_dev)
-    me = lax.axis_index("grp") * n_dev + lax.axis_index("dev")
+    my_grp, my_dev = lax.axis_index("grp"), lax.axis_index("dev")
+    me = my_grp * n_dev + my_dev
     barrier = pltpu.get_barrier_semaphore()
 
     def each(fn, first=1, last=devices):
         def body(k, carry):
-            p = lax.rem(me + k, devices)
-            fn(k, p, (p // n_dev, lax.rem(p, n_dev)))
+            g, d = partner(my_grp, lax.rem(k, n_grp), n_grp)[0], partner(my_dev, k // n_grp, n_dev)[0]
+            fn(k, g * n_dev + d, (g, d))
             return carry
         lax.fori_loop(first, last, body, 0)
 
@@ -100,14 +134,14 @@
     def big(k, p, w):
         remote(send_ref.at[p], got.at[me], s_big, r_big.at[k], w).start()
 
-    half = devices // 2
+    most_sent = devices - devices // 4
     each(lambda k, p, w: remote(part_ref.at[p], rbuf.at[me], s_rs, r_rs, w).start())
     each(lambda k, p, w: remote(meta_ref.at[p], gmeta.at[me], s_meta, r_meta, w).start())
-    each(big, 1, half)
+    each(big, 1, most_sent)
     rbuf[me] = part_ref[me]
     gmeta[me] = meta_ref[me]
 
-    here = (lax.axis_index("grp"), lax.axis_index("dev"))
+    here = (my_grp, my_dev)
     most = pl.ds(0, devices - 1)
 
     def all_of(src, dst, ssem, rsem):
@@ -116,10 +150,9 @@
     rs = all_of(part_ref, rbuf, s_rs, r_rs)
     rs.wait_recv()
     total[me] = jnp.sum(rbuf[...], axis=0)
-    each(big, half, half + half // 2)
     rs.wait_send()
     each(lambda k, p, w: remote(total.at[me], total.at[me], s_ag, r_ag, w).start())
-    each(big, half + half // 2, devices)
+    each(big, most_sent, devices)
 
     def add(values, ids):
         count = values.shape[0]
@@ -158,21 +191,20 @@
     metas.wait_recv()
 
     def arrived(k, carry):
-        source = lax.rem(me - k + devices, devices)
+        g, d = partner(my_grp, lax.rem(k, n_grp), n_grp)[1], partner(my_dev, k // n_grp, n_dev)[1]
+        source = g * n_dev + d
         remote(send_ref.at[0], got.at[source], s_big, r_big.at[k], here).wait_recv()
         add_block(source)
         return carry
 
-    lax.fori_loop(1, devices, arrived, 0)
+    lax.fori_loop(1, most_sent, arrived, 0)
     ag = all_of(total, total, s_ag, r_ag)
     ag.wait_send()
     ag.wait_recv()
     hot = ids_ref.shape[1]
     add(total[...].reshape(-1, width)[:hot], ids_ref[...] - me * rows_dev)
-    out = pltpu.make_async_copy(acc, out_ref, s_own.at[0])
-    out.start()
+    lax.fori_loop(most_sent, devices, arrived, 0)
     remote(send_ref.at[most], got.at[most], s_big, r_big.at[0], here).wait_send()
-    out.wait()
 
 
 def on_device(n_grp, n_dev, table, cold_grads, cold_owner, cold_row, hot_grads, hot_slot, hot_ids):
@@ -183,57 +215,58 @@
     hot = hot_ids.shape[0]
     slots = max(4, 2 * lookups // devices)
     tall = -(-devices // 8) * 8
-    vmem, smem, hbm = (pl.BlockSpec(memory_space=m) for m in (pltpu.VMEM, pltpu.SMEM, pl.ANY))
+    vmem, smem, anywhere, hbm = (
+        pl.BlockSpec(memory_space=m) for m in (pltpu.VMEM, pltpu.SMEM, pl.ANY, pltpu.HBM)
+    )
     f32, i32 = jnp.float32, jnp.int32
-    place, count, partial = pl.pallas_call(
-        functools.partial(plan_kernel, slots),
+    dma = pltpu.SemaphoreType.DMA
+    send, rows, count, partial = pl.pallas_call(
+        functools.partial(pack_kernel, slots),
         out_shape=(
-            jax.ShapeDtypeStruct((lookups // LANES, LANES), i32),
+            jax.ShapeDtypeStruct((devices * slots, width), f32),
+            jax.ShapeDtypeStruct((devices * slots,), i32),
             jax.ShapeDtypeStruct((tall, LANES), i32),
             jax.ShapeDtypeStruct((hot, width), f32),
         ),
-        in_specs=[vmem] * 3,
-        out_specs=(vmem,) * 3,
-        compiler_params=pltpu.CompilerParams(vmem_limit_bytes=8 * MIB),
-        name="plan",
-    )(cold_owner.reshape(-1, LANES), hot_grads, hot_slot.reshape(1, -1))
-    send, rows = pl.pallas_call(
-        pack_kernel,
-        out_shape=(
-            jax.ShapeDtypeStruct((devices * slots, width), f32),
-            jax.ShapeDtypeStruct((devices * slots,), i32),
-        ),
-        in_specs=[smem, smem, vmem],
-        out_specs=(vmem, smem),
-        compiler_params=pltpu.CompilerParams(vmem_limit_bytes=12 * MIB),
+        in_specs=[hbm] * 5,
+        out_specs=(vmem, smem, vmem, vmem),
+        scratch_shapes=[
+            pltpu.VMEM((lookups // LANES, LANES), i32),
+            pltpu.SMEM((lookups,), i32),
+            pltpu.VMEM(cold_grads.shape, f32),
+            pltpu.VMEM(hot_grads.shape, f32),
+            pltpu.VMEM((1, hot_slot.shape[0]), i32),
+            pltpu.VMEM((lookups // LANES, LANES), i32),
+            pltpu.SMEM((lookups // LANES, LANES), i32),
+            dma((6,)),
+        ],
+        compiler_params=pltpu.CompilerParams(vmem_limit_bytes=54 * MIB),
         name="pack",
-    )(place.reshape(-1), cold_row, cold_grads)
+    )(cold_owner.reshape(-1, LANES), cold_row, cold_grads, hot_grads, hot_slot.reshape(1, -1))
     lines = -(-slots // LANES)
     rows = jnp.pad(rows.reshape(devices, slots), ((0, 0), (0, lines * LANES - slots)))
-    height = -(-(lines + 1) // 8) * 8
+    height = 4 if lines < 4 else -(-(lines + 1) // 8) * 8
     meta = jnp.concatenate(
         [rows.reshape(devices, lines, LANES),
          jnp.broadcast_to(count[:devices, None, :], (devices, height - lines, LANES))], axis=1,
     )
     share = -(-hot // devices)
     partial = jnp.pad(partial, ((0, share * devices - hot), (0, 0))).reshape(devices, share, width)
-    dma = pltpu.SemaphoreType.DMA
     return pl.pallas_call(
         functools.partial(exchange_kernel, n_grp, n_dev, slots),
         out_shape=jax.ShapeDtypeStruct(table.shape, f32),
-        in_specs=[hbm, vmem, vmem, vmem, hbm],
-        out_specs=hbm,
+        in_specs=[anywhere, vmem, vmem, vmem, hbm],
+        out_specs=vmem,
         scratch_shapes=[
             pltpu.VMEM((devices, slots, width), f32),
             pltpu.VMEM(meta.shape, i32),
             pltpu.VMEM(partial.shape, f32),
             pltpu.VMEM(partial.shape, f32),
-            pltpu.VMEM(table.shape, f32),
             pltpu.VMEM((max(slots, hot), 2 * width), jnp.bfloat16),
             dma, dma((devices,)), dma, dma, dma, dma, dma, dma, dma((2,)),
         ],
         compiler_params=pltpu.CompilerParams(
-            collective_id=0, has_side_effects=True, vmem_limit_bytes=32 * MIB
+            collective_id=0, has_side_effects=True, vmem_limit_bytes=48 * MIB
         ),
         name="exchange",
     )(send.reshape(devices, slots, width), meta, partial,

time: 133 us -> 133 us (level)
  local copies, waits for them, and re-layouts: 9.63 us -> 4.32 us
  Pallas kernels: 123 us -> 126 us
    pallas_call x2 -> x1, Pallas kernels: 10.9 us -> 20.4 us  [on_device(): pl.pallas_call(functools.partial(pack_kernel, slots), out_shape=(jax.Shap...]
    unnamed x15 -> x5, local copies, waits for them, and re-layouts: 9.62 us -> 3.59 us
    pallas_call x1, Pallas kernels: 112 us -> 106 us  [on_device(): pl.pallas_call(functools.partial(exchange_kernel, n_grp, n_dev, slots), o...]
where the time goes in v4:
time: 133 us; the launch traced here: 132 us
  Pallas kernels  126 us (95%)
  local copies, waits for them, and re-layouts  4.32 us (3%)
    pallas_call x1, Pallas kernels, on_device(): pl.pallas_call(functools.partial(exchange_kernel, n_grp, n_dev, slots), o...  106 us
    pallas_call x1, Pallas kernels, on_device(): pl.pallas_call(functools.partial(pack_kernel, slots), out_shape=(jax.Shap...  20.4 us
    unnamed x5, local copies, waits for them, and re-layouts  3.59 us

profile of v4, /device:TPU:13, one launch (start us, length us, event | category | flops | bytes accessed | tf_op | source)
XLA Modules:
  0.0 131.5 jit_solution(5746603444203156628)
XLA Ops:
  0.0 20.4 %pack.1 = (f32[8192,128]{1,0:T(8,128)}, s32[8192]{0:T(1024)}, s32[32,128]{1,0:T(8,128)}, f32[256,128]{1,0:T(8,128)}) custom-call(s32[32,128]{1,0:T(8,128)} %bitcast.10, s32[4096]{0:T(1024)} %row_hbm.1, f32[4096,128]{1,0:T(8,128)} %grads_hbm.1, f32[1024,128]{1,0:T(8,128)} %hot_grads_hbm.1, s32[1,1024]{1,0:T(1,128)} %bitcast.11), custom_call_target="tpu_custom_call" | custom-call | tf_op jit(solution)/shard_map/pack/pallas_call | solution.py:223
  20.4 0.7 broadcast_in_dim.2
  21.1 0.8 pad_add_fusion.meta_ref
  21.9 0.0 copy-start
  21.9 0.9 copy-done
  22.8 0.0 copy-start.1
  22.8 0.7 copy-done.1
  23.5 106.0 %exchange.1 = f32[8192,128]{1,0:T(8,128)S(1)} custom-call(f32[32,256,128]{2,1,0:T(8,128)} %bitcast.8, s32[32,4,128]{2,1,0:T(4,128)S(1)} %pad_add_fusion.meta_ref, f32[32,8,128]{2,1,0:T(8,128)S(1)} %bitcast.6, s32[1,256]{1,0:T(1,128)S(1)} %bitcast.7, f32[8192,128]{1,0:T(8,128)} %table_ref.1), custom_call_target="tpu_custom_call" | custom-call | tf_op jit(solution)/shard_map/exchange/pallas_call | solution.py:255
  129.5 2.0 %copy.9 = f32[8192,128]{1,0:T(8,128)} copy(f32[8192,128]{1,0:T(8,128)S(1)} %exchange.1) | data formatting | bytes 8388608
Async XLA Ops:
  21.9 0.9 copy-start
  22.8 0.7 copy-start.1

commit v5 on v3

--- a/solution.py
+++ b/solution.py
@@ -66,21 +66,33 @@
     lax.fori_loop(0, grads_ref.shape[0] // step, body, 0)
 
 
+def partner(at, step, size):
+    if size & (size - 1):
+        return lax.rem(at + step, size), lax.rem(at - step + size, size)
+    mixed = 0
+    bit = 1
+    while bit < size:
+        mixed = mixed + bit * lax.rem(at // bit + step // bit, 2)
+        bit *= 2
+    return mixed, mixed
+
+
 def exchange_kernel(
-    n_grp, n_dev, slots, send_ref, meta_ref, part_ref, ids_ref, table_ref, out_ref,
-    got, gmeta, total, rbuf, acc, halves, s_big, r_big, s_meta, r_meta, s_rs, r_rs, s_ag, r_ag, s_own,
+    n_grp, n_dev, slots, send_ref, meta_ref, part_ref, ids_ref, table_ref, acc,
+    got, gmeta, total, rbuf, halves, s_big, r_big, s_meta, r_meta, s_rs, r_rs, s_ag, r_ag, s_own,
 ):
     devices = n_grp * n_dev
     width = acc.shape[1]
     rows_dev = acc.shape[0]
     tile = min(TILE, rows_dev)
-    me = lax.axis_index("grp") * n_dev + lax.axis_index("dev")
+    my_grp, my_dev = lax.axis_index("grp"), lax.axis_index("dev")
+    me = my_grp * n_dev + my_dev
     barrier = pltpu.get_barrier_semaphore()
 
     def each(fn, first=1, last=devices):
         def body(k, carry):
-            p = lax.rem(me + k, devices)
-            fn(k, p, (p // n_dev, lax.rem(p, n_dev)))
+            g, d = partner(my_grp, lax.rem(k, n_grp), n_grp)[0], partner(my_dev, k // n_grp, n_dev)[0]
+            fn(k, g * n_dev + d, (g, d))
             return carry
         lax.fori_loop(first, last, body, 0)
 
@@ -100,14 +112,14 @@
     def big(k, p, w):
         remote(send_ref.at[p], got.at[me], s_big, r_big.at[k], w).start()
 
-    half = devices // 2
+    most_sent = devices - devices // 4
     each(lambda k, p, w: remote(part_ref.at[p], rbuf.at[me], s_rs, r_rs, w).start())
     each(lambda k, p, w: remote(meta_ref.at[p], gmeta.at[me], s_meta, r_meta, w).start())
-    each(big, 1, half)
+    each(big, 1, most_sent)
     rbuf[me] = part_ref[me]
     gmeta[me] = meta_ref[me]
 
-    here = (lax.axis_index("grp"), lax.axis_index("dev"))
+    here = (my_grp, my_dev)
     most = pl.ds(0, devices - 1)
 
     def all_of(src, dst, ssem, rsem):
@@ -116,10 +128,9 @@
     rs = all_of(part_ref, rbuf, s_rs, r_rs)
     rs.wait_recv()
     total[me] = jnp.sum(rbuf[...], axis=0)
-    each(big, half, half + half // 2)
     rs.wait_send()
     each(lambda k, p, w: remote(total.at[me], total.at[me], s_ag, r_ag, w).start())
-    each(big, half + half // 2, devices)
+    each(big, most_sent, devices)
 
     def add(values, ids):
         count = values.shape[0]
@@ -158,21 +169,20 @@
     metas.wait_recv()
 
     def arrived(k, carry):
-        source = lax.rem(me - k + devices, devices)
+        g, d = partner(my_grp, lax.rem(k, n_grp), n_grp)[1], partner(my_dev, k // n_grp, n_dev)[1]
+        source = g * n_dev + d
         remote(send_ref.at[0], got.at[source], s_big, r_big.at[k], here).wait_recv()
         add_block(source)
         return carry
 
-    lax.fori_loop(1, devices, arrived, 0)
+    lax.fori_loop(1, most_sent, arrived, 0)
     ag = all_of(total, total, s_ag, r_ag)
     ag.wait_send()
     ag.wait_recv()
     hot = ids_ref.shape[1]
     add(total[...].reshape(-1, width)[:hot], ids_ref[...] - me * rows_dev)
-    out = pltpu.make_async_copy(acc, out_ref, s_own.at[0])
-    out.start()
+    lax.fori_loop(most_sent, devices, arrived, 0)
     remote(send_ref.at[most], got.at[most], s_big, r_big.at[0], here).wait_send()
-    out.wait()
 
 
 def on_device(n_grp, n_dev, table, cold_grads, cold_owner, cold_row, hot_grads, hot_slot, hot_ids):
@@ -195,6 +205,7 @@
         in_specs=[vmem] * 3,
         out_specs=(vmem,) * 3,
         compiler_params=pltpu.CompilerParams(vmem_limit_bytes=8 * MIB),
+        cost_estimate=pl.CostEstimate(flops=0, bytes_accessed=4 * MIB, transcendentals=0),
         name="plan",
     )(cold_owner.reshape(-1, LANES), hot_grads, hot_slot.reshape(1, -1))
     send, rows = pl.pallas_call(
@@ -206,11 +217,12 @@
         in_specs=[smem, smem, vmem],
         out_specs=(vmem, smem),
         compiler_params=pltpu.CompilerParams(vmem_limit_bytes=12 * MIB),
+        cost_estimate=pl.CostEstimate(flops=0, bytes_accessed=24 * MIB, transcendentals=0),
         name="pack",
     )(place.reshape(-1), cold_row, cold_grads)
     lines = -(-slots // LANES)
     rows = jnp.pad(rows.reshape(devices, slots), ((0, 0), (0, lines * LANES - slots)))
-    height = -(-(lines + 1) // 8) * 8
+    height = 4 if lines < 4 else -(-(lines + 1) // 8) * 8
     meta = jnp.concatenate(
         [rows.reshape(devices, lines, LANES),
          jnp.broadcast_to(count[:devices, None, :], (devices, height - lines, LANES))], axis=1,
@@ -222,13 +234,12 @@
         functools.partial(exchange_kernel, n_grp, n_dev, slots),
         out_shape=jax.ShapeDtypeStruct(table.shape, f32),
         in_specs=[hbm, vmem, vmem, vmem, hbm],
-        out_specs=hbm,
+        out_specs=vmem,
         scratch_shapes=[
             pltpu.VMEM((devices, slots, width), f32),
             pltpu.VMEM(meta.shape, i32),
             pltpu.VMEM(partial.shape, f32),
             pltpu.VMEM(partial.shape, f32),
-            pltpu.VMEM(table.shape, f32),
             pltpu.VMEM((max(slots, hot), 2 * width), jnp.bfloat16),
             dma, dma((devices,)), dma, dma, dma, dma, dma, dma, dma((2,)),
         ],

time: 133 us -> 129 us (0.970)
  Pallas kernels: 123 us -> 118 us
    pallas_call x1, Pallas kernels: 112 us -> 107 us  [on_device(): pl.pallas_call(functools.partial(exchange_kernel, n_grp, n_dev, slots), o...]
where the time goes in v5:
time: 129 us; the launch traced here: 128 us
  Pallas kernels  118 us (91%)
  local copies, waits for them, and re-layouts  9.64 us (7%)
    pallas_call x1, Pallas kernels, on_device(): pl.pallas_call(functools.partial(exchange_kernel, n_grp, n_dev, slots), o...  107 us
    unnamed x15, local copies, waits for them, and re-layouts  9.62 us
    pallas_call x1, Pallas kernels, on_device(): pl.pallas_call(pack_kernel, out_shape=(jax.ShapeDtypeStruct((devices * sl...  9.6 us

profile of v5, /device:TPU:13, one launch (start us, length us, event | category | flops | bytes accessed | tf_op | source)
XLA Modules:
  0.0 127.7 jit_solution(677802145214254581)
XLA Ops:
  0.0 0.0 copy-start.2
  0.0 1.0 copy-done.2
  1.0 0.0 copy-start.4
  1.0 0.7 copy-done.4
  1.8 0.0 copy-start.5
  1.8 0.7 copy-done.5
  2.4 1.3 plan.1
  3.7 0.0 copy-start.1
  3.7 1.6 %copy-done.1 = f32[4096,128]{1,0:T(8,128)S(1)} copy-done((f32[4096,128]{1,0:T(8,128)S(1)}, f32[4096,128]{1,0:T(8,128)}, u32[]{:S(2)}) %copy-start.1) | copy-done | bytes 2097176
  5.3 0.0 copy-start.3
  5.3 0.7 copy-done.3
  6.0 9.6 %pack.1 = (f32[8192,128]{1,0:T(8,128)S(1)}, s32[8192]{0:T(1024)S(1)}) custom-call(s32[4096]{0:T(1024)S(1)} %bitcast.10, s32[4096]{0:T(1024)S(1)} %copy-done.3, f32[4096,128]{1,0:T(8,128)S(1)} %copy-done.1), custom_call_target="tpu_custom_call" | custom-call | bytes 25165824 | tf_op jit(solution)/shard_map/pack/pallas_call | solution.py:211
  15.7 0.0 copy-start
  15.7 2.2 %copy-done = f32[8192,128]{1,0:T(8,128)S(1)} copy-done((f32[8192,128]{1,0:T(8,128)S(1)}, f32[8192,128]{1,0:T(8,128)}, u32[]{:S(2)}) %copy-start) | copy-done | bytes 4194328
  17.9 0.0 copy-start.6
  17.9 0.7 copy-done.6
  18.6 107.1 %exchange.1 = f32[8192,128]{1,0:T(8,128)S(1)} custom-call(f32[32,256,128]{2,1,0:T(8,128)S(1)} %bitcast.7, s32[32,4,128]{2,1,0:T(4,128)S(1)} %pad_add_fusion.meta_ref, f32[32,8,128]{2,1,0:T(8,128)S(1)} %bitcast.8, s32[1,256]{1,0:T(1,128)S(1)} %bitcast.13, f32[8192,128]{1,0:T(8,128)S(1)} %copy-done), custom_call_target="tpu_custom_call" | custom-call | tf_op jit(solution)/shard_map/exchange/pallas_call | solution.py:233
  125.7 2.0 %copy.9 = f32[8192,128]{1,0:T(8,128)} copy(f32[8192,128]{1,0:T(8,128)S(1)} %exchange.1) | data formatting | bytes 8388608
  (2 shorter events, 0.0 us)
Async XLA Ops:
  0.0 1.0 copy-start.2
  1.0 0.7 copy-start.4
  1.8 0.7 copy-start.5
  3.7 1.6 %copy-start.1 = (f32[4096,128]{1,0:T(8,128)S(1)}, f32[4096,128]{1,0:T(8,128)}, u32[]{:S(2)}) copy-start(f32[4096,128]{1,0:T(8,128)} %grads_ref.1) | copy-start | bytes 6291460
  5.3 0.7 copy-start.3
  15.7 2.2 %copy-start = (f32[8192,128]{1,0:T(8,128)S(1)}, f32[8192,128]{1,0:T(8,128)}, u32[]{:S(2)}) copy-start(f32[8192,128]{1,0:T(8,128)} %table_ref.1) | copy-start | bytes 12582916
  17.9 0.7 copy-start.6
